TPU v7x, 32 devices: a whole 2x2x4 slice. The times are simulated.
32 devices in a mesh: groups: 2 (over x), dp: 16 (over z, y, core).
Axes of the slice: x: 2, y: 2, z: 4, core: 2. Of those that a mesh axis runs over, the one named last changes fastest.
Arguments:
- queries: bfloat16 [24576, 4096], P(('groups', 'dp')), parts along dimension 0, may hold values from -120 to 120
- keys: bfloat16 [24576, 512], P(('groups', 'dp')), parts along dimension 0, may hold values from -6 to 6
- values: bfloat16 [24576, 512], P(('groups', 'dp')), parts along dimension 0, may hold values from -6 to 6
- block_counts: int32 [32], P(('groups', 'dp')), parts along dimension 0, may hold values from 0 to 6, as said below
- segment_ids: int32 [8192], P(('groups', 'dp')), parts along dimension 0, may hold values from 0 to 7, never falling along the last dimension, each value on 1 to 1024 neighbouring positions
- reward_dir: float32 [4096], replicated, may hold values from -4 to 4
Outputs:
- attn_out: bfloat16 [8192, 4096], P(('groups', 'dp')), parts along dimension 0
- rewards: float32 [16], P('groups'), parts along dimension 0
There are 2 independent parts, one for each index of `groups`. A program takes and returns all parts, laid end to end along the dimension named above; an argument that names none is the same for every part. Nothing has to cross between parts.
Inputs may be any that keep to these rules, and one draw needn't show every extreme that they name: `block_counts`: the counts sum to 2 times the number of ranks; for each rank s the counts of the ranks before s sum to between (2 * s - 2) and (2 * s + 2); some rank holds 6. `segment_ids`: positions never fall in segment number, each of the 8 responses holds 1 to 1024 positions.
All inputs are finite; a program needn't handle non-finite values.
Results may differ from a plain program's by a relative error of at most 0.0039.
The roundings to bfloat16 on the way count: a program that leaves them out, or rounds other values in their place, can miss the bound.
Values may be sent and summed in bfloat16 or wider, within the bound.
No kernel may reach another device: no remote copies, remote signals or barrier semaphores. Data moves between devices by JAX's collectives and lax.ppermute only.
A program may use at most 128 MiB of HBM per device.

v0:
```python
import jax
import jax.numpy as jnp
from jax import lax
from jax.sharding import PartitionSpec as P

D_HEAD = 128
HEADS = 32
KV_HEADS = 4
BLOCK = 128
RECV = 2
REACH = 4


def prefix_2(part, axis, combine, identity):
    place = lax.axis_index(axis)
    gathered = jax.tree.map(lambda a: lax.all_gather(a, axis), part)
    state = jax.tree.map(lambda a, e: jnp.zeros_like(a) + jnp.asarray(e, a.dtype), part, identity)

    def one(hop, state):
        return combine(
            state, jax.tree.map(lambda a: lax.dynamic_index_in_dim(a, hop, 0, False), gathered)
        )

    return lax.fori_loop(0, place, one, state)


def shifted(block, axis, distance):
    devices = range(lax.axis_size(axis))
    route = [(i - distance, i) for i in devices if i - distance in devices]
    return lax.ppermute(block, axis, route)


def shortened(shard):
    return jax.tree.map(lambda a: a.astype(jnp.bfloat16) if a.dtype == jnp.float32 else a, shard)


def attend(query_rows, key_window, value_window, allowed):
    per_group = HEADS // KV_HEADS
    row_count = query_rows.shape[0]
    score_scale = D_HEAD ** (-0.5)
    grouped = query_rows.reshape(row_count, KV_HEADS, per_group, D_HEAD)
    key_heads = key_window.reshape(-1, KV_HEADS, D_HEAD)
    value_heads = value_window.reshape(-1, KV_HEADS, D_HEAD)
    head_outs = []
    for head_index in range(KV_HEADS):
        query_head = grouped[:, head_index].reshape(row_count * per_group, D_HEAD)
        logits = (
            jnp.dot(query_head, key_heads[:, head_index].T, preferred_element_type=jnp.float32)
            * score_scale
        )
        logits = logits.reshape(row_count, per_group, -1)
        logits = jnp.where(allowed[:, None, :], logits, -1e30)
        row_max = jnp.max(logits, axis=-1, keepdims=True)
        raised = jnp.exp(logits - row_max)
        totals = jnp.sum(raised, axis=-1)
        soft_weights = raised.astype(jnp.bfloat16).reshape(row_count * per_group, -1)
        head_out = jnp.dot(
            soft_weights, value_heads[:, head_index], preferred_element_type=jnp.float32
        )
        head_out = head_out.reshape(row_count, per_group, D_HEAD) / totals[..., None]
        head_outs.append(head_out.astype(jnp.bfloat16))
    return jnp.stack(head_outs, axis=1).reshape(row_count, HEADS * D_HEAD)


def combine_all(earlier, later):
    count_a, first_a, last_a, start_a = earlier
    count_b, first_b, last_b, start_b = later
    joined = (first_b == last_b) & (last_a == first_b)
    empty_b = last_b < 0
    return (
        count_a + count_b,
        jnp.where(first_a < 0, first_b, first_a),
        jnp.where(empty_b, last_a, last_b),
        jnp.where(empty_b | joined, start_a, start_b),
    )


def shards(queries, keys, values, block_counts, segment_ids, reward_dir):
    row_count = segment_ids.shape[0]
    capacity = queries.shape[0] // BLOCK
    own_rank = lax.axis_index("dp")
    own_count = block_counts[0]
    positions = jnp.arange(row_count, dtype=jnp.int32)
    base_row = own_rank * row_count
    changed = jnp.concatenate([jnp.ones((1,), bool), segment_ids[1:] != segment_ids[:-1]])
    local_start = lax.cummax(jnp.where(changed, positions, 0), axis=0)
    summary = (
        block_counts,
        segment_ids[0:1],
        segment_ids[row_count - 1 : row_count],
        base_row + local_start[row_count - 1 : row_count],
    )
    neutral = (
        jnp.zeros((1,), jnp.int32),
        jnp.full((1,), -1, jnp.int32),
        jnp.full((1,), -1, jnp.int32),
        jnp.zeros((1,), jnp.int32),
    )
    prefix = prefix_2(summary, "dp", combine_all, neutral)
    offset = prefix[0][0]
    starts = jnp.where(segment_ids == prefix[2][0], prefix[3][0], base_row + local_start)
    following = shifted(segment_ids[0:1] + 1, "dp", -1)[0] - 1
    next_ids = jnp.concatenate([segment_ids[1:], following[None]])
    is_last = segment_ids != next_ids

    def outgoing(members, distance):
        first_pick = (own_rank + distance) * RECV - offset
        picks = first_pick + jnp.arange(RECV, dtype=jnp.int32)
        usable = (picks >= 0) & (picks < own_count)
        bounded = jnp.clip(picks, 0, capacity - 1)
        result = []
        for member in members:
            blocks = member.reshape(capacity, BLOCK, member.shape[1])
            chosen = jnp.take(blocks, bounded, axis=0)
            kept = jnp.where(usable[:, None, None], chosen, jnp.zeros_like(chosen))
            result.append(kept.reshape(row_count, member.shape[1]))
        return tuple(result)

    members = (queries, keys, values)
    arranged = outgoing(members, 0)
    for distance in (1, -1):
        parts = outgoing(members, distance)
        arrived = jax.tree.map(
            lambda part, own: part.astype(own.dtype),
            shifted(shortened(parts), "dp", distance),
            parts,
        )
        arranged = tuple((held + extra for held, extra in zip(arranged, arrived)))
    query_rows, key_rows, value_rows = arranged
    earlier = []
    carried = (key_rows, value_rows)
    for hop_index in range(REACH):
        carried = shifted((carried[0], carried[1]), "dp", 1)
        earlier.append(carried)
    earlier = earlier[::-1]
    key_window = jnp.concatenate([piece[0] for piece in earlier] + [key_rows], axis=0)
    value_window = jnp.concatenate([piece[1] for piece in earlier] + [value_rows], axis=0)
    key_window, value_window = (key_window, value_window)
    reach_rows = REACH * row_count
    key_pos = base_row - reach_rows + jnp.arange(reach_rows + row_count, dtype=jnp.int32)
    query_pos = base_row + positions
    allowed = (key_pos[None, :] >= starts[:, None]) & (key_pos[None, :] <= query_pos[:, None])
    attn_out = attend(query_rows, key_window, value_window, allowed)
    token_score = jnp.dot(attn_out.astype(jnp.float32), reward_dir, precision=lax.Precision.HIGHEST)
    response_count = lax.axis_size("dp") * 2 // REACH
    matches = (
        segment_ids[:, None] == jnp.arange(response_count, dtype=jnp.int32)[None, :]
    ) & is_last[:, None]
    partial_rewards = jnp.sum(jnp.where(matches, token_score[:, None], 0.0), axis=0)
    rewards = lax.psum(partial_rewards, "dp")
    return (attn_out, rewards)


def solution(mesh):
    return jax.shard_map(
        shards,
        mesh=mesh,
        in_specs=(
            P(("groups", "dp"), None),
            P(("groups", "dp"), None),
            P(("groups", "dp"), None),
            P(("groups", "dp")),
            P(("groups", "dp")),
            P(),
        ),
        out_specs=(P(("groups", "dp"), None), P("groups")),
        check_vma=False,
    )
```

profile of v0, /device:TPU:0, one launch (start us, length us, event | category | flops | bytes accessed | tf_op | source)
XLA Modules:
  0.0 308.4 jit_solution(2750992244555226999)
XLA Ops:
  11.2 15.8 %all-reduce.4 = (s32[16]{0:T(128)S(1)}, s32[16]{0:T(128)S(1)}, s32[16]{0:T(128)S(1)}, s32[16]{0:T(128)S(1)}) all-reduce(s32[16]{0:T(128)S(1)} %dynamic-update-slice, s32[16]{0:T(128)S(1)} %slice_dynamic-update-slice_fusion, s32[16]{0:T(128)S(1)} %get-tuple-element.116, ...), channel_id=2, replica_groups=mesh['groups'=2,'dp'=16] {'dp'}, use_global_device_ids=true, to_apply=%add | all-reduce | flops 64 | bytes 512
  30.3 5.7 %collective-permute-start.2 = (bf16[256,512]{0,1:T(8,128)(2,1)}, bf16[256,512]{0,1:T(8,128)(2,1)}, u32[]{:S(2)}, u32[]{:S(2)}) collective-permute-start(bf16[256,512]{0,1:T(8,128)(2,1)} %copy.48), channel_id=1, source_target_pairs={{0,1},{1,2},{2,3},{3,4},{4,5},{5,6},{6,7},{7,8},{8,9},{9,10},{10,1... | collective-permute-start | bytes 786440 | tf_op jit(solution)/shard_map/ppermute | solution.py:30
  36.2 11.8 %collective-permute-start.8 = (bf16[256,512]{0,1:T(8,128)(2,1)S(1)}, bf16[256,512]{0,1:T(8,128)(2,1)}, u32[]{:S(2)}, u32[]{:S(2)}) collective-permute-start(bf16[256,512]{0,1:T(8,128)(2,1)S(1)} %copy.52), channel_id=1, source_target_pairs={{0,1},{1,2},{2,3},{3,4},{4,5},{5,6},{6,7},{7,8},{8,9},{9,10},{10,1... | collective-permute-start | bytes 786440 | tf_op jit(solution)/shard_map/ppermute | solution.py:30
  54.8 3.5 %gather_fusion.2 = bf16[2,128,4096]{2,1,0:T(8,128)(2,1)S(1)} fusion(bf16[6,128,4096]{2,1,0:T(8,128)(2,1)} %bitcast.181, s32[1024]{0:T(1024)S(1)} %get-tuple-element.133), kind=kCustom, calls=%fused_computation.3.clone | custom fusion | bytes 4194312 | tf_op jit(solution)/shard_map/jit(_take)/gather | solution.py:114
  62.2 3.5 %gather_fusion.1 = bf16[2,128,4096]{2,1,0:T(8,128)(2,1)S(1)} fusion(bf16[6,128,4096]{2,1,0:T(8,128)(2,1)} %bitcast.182, s32[1024]{0:T(1024)S(1)} %get-tuple-element.134), kind=kCustom, calls=%fused_computation.2.clone | custom fusion | bytes 4194312 | tf_op jit(solution)/shard_map/jit(_take)/gather | solution.py:114
  68.3 7.0 %collective-permute-start.10 = (bf16[256,512]{0,1:T(8,128)(2,1)S(1)}, bf16[256,512]{0,1:T(8,128)(2,1)S(1)}, u32[]{:S(2)}, u32[]{:S(2)}) collective-permute-start(bf16[256,512]{0,1:T(8,128)(2,1)S(1)} %add_add_fusion), channel_id=1, source_target_pairs={{0,1},{1,2},{2,3},{3,4},{4,5},{5,6},{6,7},{7,8},{8,9},{9,10},{10,1... | collective-permute-start | bytes 786440 | tf_op jit(solution)/shard_map/ppermute | solution.py:30
  76.9 3.5 %gather_fusion = bf16[2,128,4096]{2,1,0:T(8,128)(2,1)S(1)} fusion(bf16[6,128,4096]{2,1,0:T(8,128)(2,1)} %bitcast.183, s32[1024]{0:T(1024)S(1)} %pad_clamp_fusion.2), kind=kCustom, calls=%fused_computation.clone | custom fusion | bytes 4194312 | tf_op jit(solution)/shard_map/jit(_take)/gather | solution.py:114
  80.5 12.0 %collective-permute-start = (bf16[256,4096]{1,0:T(8,128)(2,1)}, bf16[256,4096]{1,0:T(8,128)(2,1)}, u32[]{:S(2)}, u32[]{:S(2)}) collective-permute-start(bf16[256,4096]{1,0:T(8,128)(2,1)} %bitcast.185), channel_id=1, source_target_pairs={{0,1},{1,2},{2,3},{3,4},{4,5},{5,6},{6,7},{7,8},{8,9},{9,10},{10,1... | collective-permute-start | bytes 6291464 | tf_op jit(solution)/shard_map/ppermute | solution.py:30
  93.5 4.9 %collective-permute-start.4 = (bf16[256,512]{0,1:T(8,128)(2,1)S(1)}, bf16[256,512]{0,1:T(8,128)(2,1)S(1)}, u32[]{:S(2)}, u32[]{:S(2)}) collective-permute-start(bf16[256,512]{0,1:T(8,128)(2,1)S(1)} %add_add_fusion.1), channel_id=1, source_target_pairs={{0,1},{1,2},{2,3},{3,4},{4,5},{5,6},{6,7},{7,8},{8,9},{9,10},{10,1... | collective-permute-start | bytes 786440 | tf_op jit(solution)/shard_map/ppermute | solution.py:30
  98.5 10.7 %collective-permute-start.11 = (bf16[256,512]{0,1:T(8,128)(2,1)S(1)}, bf16[256,512]{0,1:T(8,128)(2,1)S(1)}, u32[]{:S(2)}, u32[]{:S(2)}) collective-permute-start(bf16[256,512]{0,1:T(8,128)(2,1)S(1)} %collective-permute-done.10), channel_id=1, source_target_pairs={{0,1},{1,2},{2,3},{3,4},{4,5},{5,6},{6,7},{7,8},{8,9},{9,10},{10,1... | collective-permute-start | bytes 786440 | tf_op jit(solution)/shard_map/ppermute | solution.py:30
  110.8 32.0 %collective-permute-start.5 = (bf16[256,512]{0,1:T(8,128)(2,1)S(1)}, bf16[256,512]{0,1:T(8,128)(2,1)S(1)}, u32[]{:S(2)}, u32[]{:S(2)}) collective-permute-start(bf16[256,512]{0,1:T(8,128)(2,1)S(1)} %collective-permute-done.4), channel_id=1, source_target_pairs={{0,1},{1,2},{2,3},{3,4},{4,5},{5,6},{6,7},{7,8},{8,9},{9,10},{10,1... | collective-permute-start | bytes 786440 | tf_op jit(solution)/shard_map/ppermute | solution.py:30
  142.9 4.4 %collective-permute-start.12 = (bf16[256,512]{0,1:T(8,128)(2,1)S(1)}, bf16[256,512]{0,1:T(8,128)(2,1)S(1)}, u32[]{:S(2)}, u32[]{:S(2)}) collective-permute-start(bf16[256,512]{0,1:T(8,128)(2,1)S(1)} %collective-permute-done.11), channel_id=1, source_target_pairs={{0,1},{1,2},{2,3},{3,4},{4,5},{5,6},{6,7},{7,8},{8,9},{9,10},{10,1... | collective-permute-start | bytes 786440 | tf_op jit(solution)/shard_map/ppermute | solution.py:30
  150.5 4.4 %collective-permute-start.13 = (bf16[256,512]{0,1:T(8,128)(2,1)S(1)}, bf16[256,512]{0,1:T(8,128)(2,1)S(1)}, u32[]{:S(2)}, u32[]{:S(2)}) collective-permute-start(bf16[256,512]{0,1:T(8,128)(2,1)S(1)} %collective-permute-done.12), channel_id=1, source_target_pairs={{0,1},{1,2},{2,3},{3,4},{4,5},{5,6},{6,7},{7,8},{8,9},{9,10},{10,1... | collective-permute-start | bytes 786440 | tf_op jit(solution)/shard_map/ppermute | solution.py:30
  156.1 21.6 %collective-permute-start.7 = (bf16[256,512]{0,1:T(8,128)(2,1)S(1)}, bf16[256,512]{0,1:T(8,128)(2,1)S(1)}, u32[]{:S(2)}, u32[]{:S(2)}) collective-permute-start(bf16[256,512]{0,1:T(8,128)(2,1)S(1)} %collective-permute-done.6), channel_id=1, source_target_pairs={{0,1},{1,2},{2,3},{3,4},{4,5},{5,6},{6,7},{7,8},{8,9},{9,10},{10,1... | collective-permute-start | bytes 786440 | tf_op jit(solution)/shard_map/ppermute | solution.py:30
  185.1 5.6 %fusion.65 = (f32[2048]{0:T(1024)S(1)}, f32[2048,1280]{1,0:T(8,128)}) fusion(bf16[1280,4,128]{0,2,1:T(8,128)(2,1)S(1)} %bitcast.187, bf16[256,4,8,128]{3,2,1,0:T(8,128)(2,1)S(1)} %bitcast.177, pred[256,1280]{1,0:T(8,128)(4,1)S(1)} %compare_and_fusion), kind=kOutput, calls=%fused_computation.122 | convolution fusion | flops 678950912 | bytes 11673600 | tf_op jit(solution)/shard_map/dot_general | solution.py:48
  190.8 5.3 %fusion.66 = (f32[2048]{0:T(1024)S(1)}, f32[2048,1280]{1,0:T(8,128)}) fusion(bf16[1280,4,128]{0,2,1:T(8,128)(2,1)S(1)} %bitcast.188, bf16[256,4,8,128]{3,2,1,0:T(8,128)(2,1)S(1)} %bitcast.178, pred[256,1280]{1,0:T(8,128)(4,1)S(1)} %compare_and_fusion), kind=kOutput, calls=%fused_computation.123 | convolution fusion | flops 678950912 | bytes 11673600 | tf_op jit(solution)/shard_map/dot_general | solution.py:48
  196.1 5.1 %fusion.67 = (f32[2048]{0:T(1024)S(1)}, f32[2048,1280]{1,0:T(8,128)}) fusion(bf16[1280,4,128]{0,2,1:T(8,128)(2,1)S(1)} %bitcast.189, bf16[256,4,8,128]{3,2,1,0:T(8,128)(2,1)S(1)} %bitcast.179, pred[256,1280]{1,0:T(8,128)(4,1)S(1)} %compare_and_fusion), kind=kOutput, calls=%fused_computation.124 | convolution fusion | flops 678950912 | bytes 11673600 | tf_op jit(solution)/shard_map/dot_general | solution.py:48
  203.1 5.7 %fusion.4 = f32[2048]{0:T(1024)S(1)} fusion(f32[2048,1280]{1,0:T(8,128)} %get-tuple-element.126, f32[2048]{0:T(1024)S(1)} %get-tuple-element.125), kind=kLoop, calls=%fused_computation.25 | loop fusion | flops 5240832 | bytes 10502144 | tf_op jit(solution)/shard_map/reduce_sum | solution.py:55
  208.9 6.0 %fusion.58 = bf16[256,1,8,128]{3,2,0,1:T(8,128)(2,1)S(1)} fusion(f32[2048,1280]{1,0:T(8,128)} %copy-done.2, f32[2048]{0:T(1024)S(1)} %get-tuple-element.123, f32[256,8]{1,0:T(8,128)S(1)} %div.49, bf16[1280,4,128]{0,2,1:T(8,128)(2,1)S(1)} %bitcast.199), kind=kOutput, calls=%fused_computation.59 | convolution fusion | flops 676855808 | bytes 11476992 | tf_op jit(solution)/shard_map/dot_general | solution.py:57
  214.9 6.0 %fusion.49 = bf16[256,1,8,128]{3,2,0,1:T(8,128)(2,1)S(1)} fusion(f32[2048,1280]{1,0:T(8,128)} %get-tuple-element.126, f32[2048]{0:T(1024)S(1)} %get-tuple-element.125, f32[256,8]{1,0:T(8,128)S(1)} %div.46, bf16[1280,4,128]{0,2,1:T(8,128)(2,1)S(1)} %bitcast.200), kind=kOutput, calls=%fused_computation.56 | convolution fusion | flops 676855808 | bytes 11476992 | tf_op jit(solution)/shard_map/dot_general | solution.py:57
  222.8 5.8 %fusion.40 = bf16[256,1,8,128]{3,2,0,1:T(8,128)(2,1)S(1)} fusion(f32[2048,1280]{1,0:T(8,128)} %get-tuple-element.128, f32[2048]{0:T(1024)S(1)} %get-tuple-element.127, f32[256,8]{1,0:T(8,128)S(1)} %div.43, bf16[1280,4,128]{0,2,1:T(8,128)(2,1)S(1)} %bitcast.201), kind=kOutput, calls=%fused_computation.53 | convolution fusion | flops 676855808 | bytes 11476992 | tf_op jit(solution)/shard_map/dot_general | solution.py:57
  228.6 5.9 %fusion = f32[2048]{0:T(1024)S(1)} fusion(f32[2048,1280]{1,0:T(8,128)} %get-tuple-element.130, f32[2048]{0:T(1024)S(1)} %get-tuple-element.129), kind=kLoop, calls=%fused_computation.21 | loop fusion | flops 5240832 | bytes 10502144 | tf_op jit(solution)/shard_map/reduce_sum | solution.py:55
  234.7 5.8 %fusion.31 = bf16[256,1,8,128]{3,2,0,1:T(8,128)(2,1)S(1)} fusion(f32[2048,1280]{1,0:T(8,128)} %get-tuple-element.130, f32[2048]{0:T(1024)S(1)} %get-tuple-element.129, f32[256,8]{1,0:T(8,128)S(1)} %div.40, bf16[1280,4,128]{0,2,1:T(8,128)(2,1)S(1)} %bitcast.202), kind=kOutput, calls=%fused_computation.50 | convolution fusion | flops 676855808 | bytes 11476992 | tf_op jit(solution)/shard_map/dot_general | solution.py:57
  249.0 59.4 %psum.7 = f32[8]{0:T(128)} all-reduce(f32[8]{0:T(128)S(1)} %select_reduce_fusion), channel_id=1, replica_groups=mesh['groups'=2,'dp'=16] {'dp'}, use_global_device_ids=true, to_apply=%region_13.16 | all-reduce | flops 8 | bytes 64 | tf_op jit(solution)/shard_map/psum | solution.py:150
  (124 shorter events, 53.7 us)
Async XLA Ops:
  0.6 26.4 %copy-start = (bf16[768,512]{1,0:T(8,128)(2,1)S(1)}, bf16[768,512]{1,0:T(8,128)(2,1)}, u32[]{:S(2)}) copy-start(bf16[768,512]{1,0:T(8,128)(2,1)} %param.14) | copy-start | bytes 2359300
  4.5 150.8 %collective-permute-start.14 = (s32[1]{0:T(128)}, s32[1]{0:T(128)}, u32[]{:S(2)}, u32[]{:S(2)}) collective-permute-start(s32[1]{0:T(128)} %add.136), channel_id=1, source_target_pairs={{1,0},{2,1},{3,2},{4,3},{5,4},{6,5},{7,6},{8,7},{9,8},{10,9},{11,1... | collective-permute-start | bytes 20 | tf_op jit(solution)/shard_map/ppermute | solution.py:30
  30.3 50.2 %collective-permute-start.2 = (bf16[256,512]{0,1:T(8,128)(2,1)}, bf16[256,512]{0,1:T(8,128)(2,1)}, u32[]{:S(2)}, u32[]{:S(2)}) collective-permute-start(bf16[256,512]{0,1:T(8,128)(2,1)} %copy.48), channel_id=1, source_target_pairs={{0,1},{1,2},{2,3},{3,4},{4,5},{5,6},{6,7},{7,8},{8,9},{9,10},{10,1... | collective-permute-start | bytes 786440 | tf_op jit(solution)/shard_map/ppermute | solution.py:30
  36.2 29.7 %collective-permute-start.8 = (bf16[256,512]{0,1:T(8,128)(2,1)S(1)}, bf16[256,512]{0,1:T(8,128)(2,1)}, u32[]{:S(2)}, u32[]{:S(2)}) collective-permute-start(bf16[256,512]{0,1:T(8,128)(2,1)S(1)} %copy.52), channel_id=1, source_target_pairs={{0,1},{1,2},{2,3},{3,4},{4,5},{5,6},{6,7},{7,8},{8,9},{9,10},{10,1... | collective-permute-start | bytes 786440 | tf_op jit(solution)/shard_map/ppermute | solution.py:30
  51.3 41.2 %collective-permute-start.3 = (bf16[256,512]{0,1:T(8,128)(2,1)}, bf16[256,512]{0,1:T(8,128)(2,1)}, u32[]{:S(2)}, u32[]{:S(2)}) collective-permute-start(bf16[256,512]{0,1:T(8,128)(2,1)} %copy.50), channel_id=1, source_target_pairs={{1,0},{2,1},{3,2},{4,3},{5,4},{6,5},{7,6},{8,7},{9,8},{10,9},{11,1... | collective-permute-start | bytes 786440 | tf_op jit(solution)/shard_map/ppermute | solution.py:30
  53.4 13.8 %collective-permute-start.9 = (bf16[256,512]{0,1:T(8,128)(2,1)}, bf16[256,512]{0,1:T(8,128)(2,1)}, u32[]{:S(2)}, u32[]{:S(2)}) collective-permute-start(bf16[256,512]{0,1:T(8,128)(2,1)} %copy.54), channel_id=1, source_target_pairs={{1,0},{2,1},{3,2},{4,3},{5,4},{6,5},{7,6},{8,7},{9,8},{10,9},{11,1... | collective-permute-start | bytes 786440 | tf_op jit(solution)/shard_map/ppermute | solution.py:30
  65.9 113.2 %collective-permute-start.1 = (bf16[256,4096]{1,0:T(8,128)(2,1)}, bf16[256,4096]{1,0:T(8,128)(2,1)}, u32[]{:S(2)}, u32[]{:S(2)}) collective-permute-start(bf16[256,4096]{1,0:T(8,128)(2,1)} %bitcast.184), channel_id=1, source_target_pairs={{1,0},{2,1},{3,2},{4,3},{5,4},{6,5},{7,6},{8,7},{9,8},{10,9},{11,1... | collective-permute-start | bytes 6291464 | tf_op jit(solution)/shard_map/ppermute | solution.py:30
  68.3 30.2 %collective-permute-start.10 = (bf16[256,512]{0,1:T(8,128)(2,1)S(1)}, bf16[256,512]{0,1:T(8,128)(2,1)S(1)}, u32[]{:S(2)}, u32[]{:S(2)}) collective-permute-start(bf16[256,512]{0,1:T(8,128)(2,1)S(1)} %add_add_fusion), channel_id=1, source_target_pairs={{0,1},{1,2},{2,3},{3,4},{4,5},{5,6},{6,7},{7,8},{8,9},{9,10},{10,1... | collective-permute-start | bytes 786440 | tf_op jit(solution)/shard_map/ppermute | solution.py:30
  80.5 98.7 %collective-permute-start = (bf16[256,4096]{1,0:T(8,128)(2,1)}, bf16[256,4096]{1,0:T(8,128)(2,1)}, u32[]{:S(2)}, u32[]{:S(2)}) collective-permute-start(bf16[256,4096]{1,0:T(8,128)(2,1)} %bitcast.185), channel_id=1, source_target_pairs={{0,1},{1,2},{2,3},{3,4},{4,5},{5,6},{6,7},{7,8},{8,9},{9,10},{10,1... | collective-permute-start | bytes 6291464 | tf_op jit(solution)/shard_map/ppermute | solution.py:30
  93.5 53.7 %copy-start.9 = (s32[256]{0:T(256)S(1)}, s32[256]{0:T(256)}, u32[]{:S(2)}) copy-start(s32[256]{0:T(256)} %param.16) | copy-start | bytes 3076
  93.5 17.2 %collective-permute-start.4 = (bf16[256,512]{0,1:T(8,128)(2,1)S(1)}, bf16[256,512]{0,1:T(8,128)(2,1)S(1)}, u32[]{:S(2)}, u32[]{:S(2)}) collective-permute-start(bf16[256,512]{0,1:T(8,128)(2,1)S(1)} %add_add_fusion.1), channel_id=1, source_target_pairs={{0,1},{1,2},{2,3},{3,4},{4,5},{5,6},{6,7},{7,8},{8,9},{9,10},{10,1... | collective-permute-start | bytes 786440 | tf_op jit(solution)/shard_map/ppermute | solution.py:30
  98.5 44.4 %collective-permute-start.11 = (bf16[256,512]{0,1:T(8,128)(2,1)S(1)}, bf16[256,512]{0,1:T(8,128)(2,1)S(1)}, u32[]{:S(2)}, u32[]{:S(2)}) collective-permute-start(bf16[256,512]{0,1:T(8,128)(2,1)S(1)} %collective-permute-done.10), channel_id=1, source_target_pairs={{0,1},{1,2},{2,3},{3,4},{4,5},{5,6},{6,7},{7,8},{8,9},{9,10},{10,1... | collective-permute-start | bytes 786440 | tf_op jit(solution)/shard_map/ppermute | solution.py:30
  110.8 39.7 %copy-start.4 = (bf16[256,512]{0,1:T(8,128)(2,1)}, bf16[256,512]{0,1:T(8,128)(2,1)S(1)}, u32[]{:S(2)}) copy-start(bf16[256,512]{0,1:T(8,128)(2,1)S(1)} %collective-permute-done.4) | copy-start | bytes 786436
  110.8 36.5 %collective-permute-start.5 = (bf16[256,512]{0,1:T(8,128)(2,1)S(1)}, bf16[256,512]{0,1:T(8,128)(2,1)S(1)}, u32[]{:S(2)}, u32[]{:S(2)}) collective-permute-start(bf16[256,512]{0,1:T(8,128)(2,1)S(1)} %collective-permute-done.4), channel_id=1, source_target_pairs={{0,1},{1,2},{2,3},{3,4},{4,5},{5,6},{6,7},{7,8},{8,9},{9,10},{10,1... | collective-permute-start | bytes 786440 | tf_op jit(solution)/shard_map/ppermute | solution.py:30
  142.9 7.7 %collective-permute-start.12 = (bf16[256,512]{0,1:T(8,128)(2,1)S(1)}, bf16[256,512]{0,1:T(8,128)(2,1)S(1)}, u32[]{:S(2)}, u32[]{:S(2)}) collective-permute-start(bf16[256,512]{0,1:T(8,128)(2,1)S(1)} %collective-permute-done.11), channel_id=1, source_target_pairs={{0,1},{1,2},{2,3},{3,4},{4,5},{5,6},{6,7},{7,8},{8,9},{9,10},{10,1... | collective-permute-start | bytes 786440 | tf_op jit(solution)/shard_map/ppermute | solution.py:30
  147.3 8.8 %collective-permute-start.6 = (bf16[256,512]{0,1:T(8,128)(2,1)S(1)}, bf16[256,512]{0,1:T(8,128)(2,1)S(1)}, u32[]{:S(2)}, u32[]{:S(2)}) collective-permute-start(bf16[256,512]{0,1:T(8,128)(2,1)S(1)} %collective-permute-done.5), channel_id=1, source_target_pairs={{0,1},{1,2},{2,3},{3,4},{4,5},{5,6},{6,7},{7,8},{8,9},{9,10},{10,1... | collective-permute-start | bytes 786440 | tf_op jit(solution)/shard_map/ppermute | solution.py:30
  150.5 27.2 %collective-permute-start.13 = (bf16[256,512]{0,1:T(8,128)(2,1)S(1)}, bf16[256,512]{0,1:T(8,128)(2,1)S(1)}, u32[]{:S(2)}, u32[]{:S(2)}) collective-permute-start(bf16[256,512]{0,1:T(8,128)(2,1)S(1)} %collective-permute-done.12), channel_id=1, source_target_pairs={{0,1},{1,2},{2,3},{3,4},{4,5},{5,6},{6,7},{7,8},{8,9},{9,10},{10,1... | collective-permute-start | bytes 786440 | tf_op jit(solution)/shard_map/ppermute | solution.py:30
  156.1 23.0 %copy-start.5 = (bf16[256,512]{0,1:T(8,128)(2,1)S(1)}, bf16[256,512]{0,1:T(8,128)(2,1)}, u32[]{:S(2)}) copy-start(bf16[256,512]{0,1:T(8,128)(2,1)} %copy-done.4) | copy-start | bytes 786436
  156.1 22.9 %collective-permute-start.7 = (bf16[256,512]{0,1:T(8,128)(2,1)S(1)}, bf16[256,512]{0,1:T(8,128)(2,1)S(1)}, u32[]{:S(2)}, u32[]{:S(2)}) collective-permute-start(bf16[256,512]{0,1:T(8,128)(2,1)S(1)} %collective-permute-done.6), channel_id=1, source_target_pairs={{0,1},{1,2},{2,3},{3,4},{4,5},{5,6},{6,7},{7,8},{8,9},{9,10},{10,1... | collective-permute-start | bytes 786440 | tf_op jit(solution)/shard_map/ppermute | solution.py:30
  179.0 35.9 %copy-start.7 = (bf16[1280,512]{0,1:T(8,128)(2,1)}, bf16[1280,512]{0,1:T(8,128)(2,1)S(1)}, u32[]{:S(2)}) copy-start(bf16[1280,512]{0,1:T(8,128)(2,1)S(1)} %constant_dynamic-update-slice_fusion.5) | copy-start | bytes 3932164
  185.1 16.1 %copy-start.2 = (f32[2048,1280]{1,0:T(8,128)}, f32[2048,1280]{1,0:T(8,128)S(1)}, u32[]{:S(2)}) copy-start(f32[2048,1280]{1,0:T(8,128)S(1)} %get-tuple-element.124) | copy-start | bytes 31457284
  208.9 12.0 %slice-start = ((s8[10485760]{0:T(1024)(128)(4,1)}), s8[4194304]{0:T(1024)(128)(4,1)S(1)}, s32[]{:S(2)}) async-start(s8[10485760]{0:T(1024)(128)(4,1)} %bitcast.172), calls=%async_computation | async-start | bytes 8388608
  208.9 12.0 %slice-start.1 = ((s8[10485760]{0:T(1024)(128)(4,1)}), s8[4194304]{0:T(1024)(128)(4,1)S(1)}, s32[]{:S(2)}) async-start(s8[10485760]{0:T(1024)(128)(4,1)} %bitcast.172), calls=%async_computation.1 | async-start | bytes 8388608
  246.0 62.4 %copy-start.1 = (bf16[768,512]{1,0:T(8,128)(2,1)S(1)}, bf16[768,512]{1,0:T(8,128)(2,1)}, u32[]{:S(2)}) copy-start(bf16[768,512]{1,0:T(8,128)(2,1)} %param.14) | copy-start | bytes 2359300
  (5 other events, 20.3 us)
where the time goes:
time: 310 us; the launch traced here: 308 us
  starting transfers between devices  123 us (40%)
  blocking collectives  75.2 us (24%)
  matrix products  43.2 us (14%)
  local copies, waits for them, and re-layouts  34.3 us (11%)
  other arithmetic  29.4 us (9%)
  between operations  3.36 us (1%)
    ppermute x15, starting transfers between devices, shifted(): return lax.ppermute(block, axis, route)  123 us
    psum x1, blocking collectives, shards(): rewards = lax.psum(partial_rewards, 'dp')  59.4 us
    dot_general x4, matrix products, attend(): jnp.dot(soft_weights, value_heads[:, head_index], preferred_element_type=...  23.6 us
    dot_general x4, matrix products, attend(): jnp.dot(query_head, key_heads[:, head_index].T, preferred_element_type=jn...  18.7 us
    gather x9, local copies, waits for them, and re-layouts, outgoing(): chosen = jnp.take(blocks, bounded, axis=0)  17.2 us
    unnamed x1, blocking collectives  15.8 us
    reduce_sum x4, other arithmetic, attend(): totals = jnp.sum(raised, axis=-1)  15.1 us
    unnamed x45, local copies, waits for them, and re-layouts  8.63 us
  transfers between devices with their start and end apart: 15, of which 0 were waited for; matrix products, arithmetic and copies ran while one was open for 11% of the time, Pallas kernels for 0%

commit v1 on v0

--- a/solution.py
+++ b/solution.py
@@ -9,6 +9,14 @@
 BLOCK = 128
 RECV = 2
 REACH = 4
+
+
+def sum_by_hops(x, axis):
+    size, acc = (lax.axis_size(axis), x)
+    for far in [1 << k for k in range(size.bit_length() - 1)]:
+        pairs = [(i, i ^ far) for i in range(size)]
+        acc = acc + lax.ppermute(acc, axis, pairs)
+    return acc
 
 
 def prefix_2(part, axis, combine, identity):
@@ -147,7 +155,7 @@
         segment_ids[:, None] == jnp.arange(response_count, dtype=jnp.int32)[None, :]
     ) & is_last[:, None]
     partial_rewards = jnp.sum(jnp.where(matches, token_score[:, None], 0.0), axis=0)
-    rewards = lax.psum(partial_rewards, "dp")
+    rewards = sum_by_hops(partial_rewards, "dp")
     return (attn_out, rewards)
 
 

time: 310 us -> 293 us (0.945)
  blocking collectives: 75.2 us -> 15.8 us
  starting transfers between devices: 123 us -> 159 us
  waiting for transfers between devices: 0.04 us -> 5.49 us
    psum x1 -> x0, blocking collectives: 59.4 us -> none  [shards(): rewards = lax.psum(partial_rewards, 'dp')]
    ppermute x0 -> x4, starting transfers between devices: none -> 36.7 us  [sum_by_hops(): acc = acc + lax.ppermute(acc, axis, pairs)]
    ppermute x0 -> x4, waiting for transfers between devices: none -> 5.46 us  [sum_by_hops(): acc = acc + lax.ppermute(acc, axis, pairs)]
  transfers between devices with their start and end apart: 15 -> 19, of which waited for: 0 -> 4; matrix products, arithmetic and copies ran while one was open for 11% -> 12% of each run, Pallas kernels for 0% -> 0%
where the time goes in v1:
time: 293 us; the launch traced here: 291 us
  starting transfers between devices  159 us (54%)
  matrix products  43.2 us (15%)
  local copies, waits for them, and re-layouts  34.4 us (12%)
  other arithmetic  30 us (10%)
  blocking collectives  15.8 us (5%)
  waiting for transfers between devices  5.49 us (2%)
  between operations  3.3 us (1%)
    ppermute x15, starting transfers between devices, shifted(): return lax.ppermute(block, axis, route)  122 us
    ppermute x4, starting transfers between devices, sum_by_hops(): acc = acc + lax.ppermute(acc, axis, pairs)  36.7 us
    dot_general x4, matrix products, attend(): jnp.dot(soft_weights, value_heads[:, head_index], preferred_element_type=...  23.6 us
    dot_general x4, matrix products, attend(): jnp.dot(query_head, key_heads[:, head_index].T, preferred_element_type=jn...  18.7 us
    gather x9, local copies, waits for them, and re-layouts, outgoing(): chosen = jnp.take(blocks, bounded, axis=0)  17.2 us
    unnamed x1, blocking collectives  15.8 us
    reduce_sum x4, other arithmetic, attend(): totals = jnp.sum(raised, axis=-1)  15.1 us
    unnamed x45, local copies, waits for them, and re-layouts  8.68 us
  transfers between devices with their start and end apart: 19, of which 4 were waited for; matrix products, arithmetic and copies ran while one was open for 12% of the time, Pallas kernels for 0%

profile of v1, /device:TPU:0, one launch (start us, length us, event | category | flops | bytes accessed | tf_op | source)
XLA Modules:
  0.0 291.2 jit_solution(7640645194891241703)
XLA Ops:
  11.2 15.8 %all-reduce.4 = (s32[16]{0:T(128)S(1)}, s32[16]{0:T(128)S(1)}, s32[16]{0:T(128)S(1)}, s32[16]{0:T(128)S(1)}) all-reduce(s32[16]{0:T(128)S(1)} %dynamic-update-slice, s32[16]{0:T(128)S(1)} %slice_dynamic-update-slice_fusion, s32[16]{0:T(128)S(1)} %get-tuple-element.116, ...), channel_id=2, replica_groups=mesh['groups'=2,'dp'=16] {'dp'}, use_global_device_ids=true, to_apply=%add | all-reduce | flops 64 | bytes 512
  30.4 5.8 %collective-permute-start.2 = (bf16[256,512]{0,1:T(8,128)(2,1)}, bf16[256,512]{0,1:T(8,128)(2,1)}, u32[]{:S(2)}, u32[]{:S(2)}) collective-permute-start(bf16[256,512]{0,1:T(8,128)(2,1)} %copy.48), channel_id=1, source_target_pairs={{0,1},{1,2},{2,3},{3,4},{4,5},{5,6},{6,7},{7,8},{8,9},{9,10},{10,1... | collective-permute-start | bytes 786440 | tf_op jit(solution)/shard_map/ppermute | solution.py:38
  36.3 11.7 %collective-permute-start.8 = (bf16[256,512]{0,1:T(8,128)(2,1)S(1)}, bf16[256,512]{0,1:T(8,128)(2,1)}, u32[]{:S(2)}, u32[]{:S(2)}) collective-permute-start(bf16[256,512]{0,1:T(8,128)(2,1)S(1)} %copy.52), channel_id=1, source_target_pairs={{0,1},{1,2},{2,3},{3,4},{4,5},{5,6},{6,7},{7,8},{8,9},{9,10},{10,1... | collective-permute-start | bytes 786440 | tf_op jit(solution)/shard_map/ppermute | solution.py:38
  68.3 6.9 %collective-permute-start.10 = (bf16[256,512]{0,1:T(8,128)(2,1)S(1)}, bf16[256,512]{0,1:T(8,128)(2,1)S(1)}, u32[]{:S(2)}, u32[]{:S(2)}) collective-permute-start(bf16[256,512]{0,1:T(8,128)(2,1)S(1)} %add_add_fusion), channel_id=1, source_target_pairs={{0,1},{1,2},{2,3},{3,4},{4,5},{5,6},{6,7},{7,8},{8,9},{9,10},{10,1... | collective-permute-start | bytes 786440 | tf_op jit(solution)/shard_map/ppermute | solution.py:38
  80.4 12.0 %collective-permute-start = (bf16[256,4096]{1,0:T(8,128)(2,1)}, bf16[256,4096]{1,0:T(8,128)(2,1)}, u32[]{:S(2)}, u32[]{:S(2)}) collective-permute-start(bf16[256,4096]{1,0:T(8,128)(2,1)} %bitcast.185), channel_id=1, source_target_pairs={{0,1},{1,2},{2,3},{3,4},{4,5},{5,6},{6,7},{7,8},{8,9},{9,10},{10,1... | collective-permute-start | bytes 6291464 | tf_op jit(solution)/shard_map/ppermute | solution.py:38
  93.5 4.8 %collective-permute-start.4 = (bf16[256,512]{0,1:T(8,128)(2,1)S(1)}, bf16[256,512]{0,1:T(8,128)(2,1)S(1)}, u32[]{:S(2)}, u32[]{:S(2)}) collective-permute-start(bf16[256,512]{0,1:T(8,128)(2,1)S(1)} %add_add_fusion.1), channel_id=1, source_target_pairs={{0,1},{1,2},{2,3},{3,4},{4,5},{5,6},{6,7},{7,8},{8,9},{9,10},{10,1... | collective-permute-start | bytes 786440 | tf_op jit(solution)/shard_map/ppermute | solution.py:38
  98.3 10.6 %collective-permute-start.11 = (bf16[256,512]{0,1:T(8,128)(2,1)S(1)}, bf16[256,512]{0,1:T(8,128)(2,1)S(1)}, u32[]{:S(2)}, u32[]{:S(2)}) collective-permute-start(bf16[256,512]{0,1:T(8,128)(2,1)S(1)} %collective-permute-done.10), channel_id=1, source_target_pairs={{0,1},{1,2},{2,3},{3,4},{4,5},{5,6},{6,7},{7,8},{8,9},{9,10},{10,1... | collective-permute-start | bytes 786440 | tf_op jit(solution)/shard_map/ppermute | solution.py:38
  110.6 32.0 %collective-permute-start.5 = (bf16[256,512]{0,1:T(8,128)(2,1)S(1)}, bf16[256,512]{0,1:T(8,128)(2,1)S(1)}, u32[]{:S(2)}, u32[]{:S(2)}) collective-permute-start(bf16[256,512]{0,1:T(8,128)(2,1)S(1)} %collective-permute-done.4), channel_id=1, source_target_pairs={{0,1},{1,2},{2,3},{3,4},{4,5},{5,6},{6,7},{7,8},{8,9},{9,10},{10,1... | collective-permute-start | bytes 786440 | tf_op jit(solution)/shard_map/ppermute | solution.py:38
  142.7 4.4 %collective-permute-start.12 = (bf16[256,512]{0,1:T(8,128)(2,1)S(1)}, bf16[256,512]{0,1:T(8,128)(2,1)S(1)}, u32[]{:S(2)}, u32[]{:S(2)}) collective-permute-start(bf16[256,512]{0,1:T(8,128)(2,1)S(1)} %collective-permute-done.11), channel_id=1, source_target_pairs={{0,1},{1,2},{2,3},{3,4},{4,5},{5,6},{6,7},{7,8},{8,9},{9,10},{10,1... | collective-permute-start | bytes 786440 | tf_op jit(solution)/shard_map/ppermute | solution.py:38
  150.4 4.4 %collective-permute-start.13 = (bf16[256,512]{0,1:T(8,128)(2,1)S(1)}, bf16[256,512]{0,1:T(8,128)(2,1)S(1)}, u32[]{:S(2)}, u32[]{:S(2)}) collective-permute-start(bf16[256,512]{0,1:T(8,128)(2,1)S(1)} %collective-permute-done.12), channel_id=1, source_target_pairs={{0,1},{1,2},{2,3},{3,4},{4,5},{5,6},{6,7},{7,8},{8,9},{9,10},{10,1... | collective-permute-start | bytes 786440 | tf_op jit(solution)/shard_map/ppermute | solution.py:38
  155.9 21.4 %collective-permute-start.7 = (bf16[256,512]{0,1:T(8,128)(2,1)S(1)}, bf16[256,512]{0,1:T(8,128)(2,1)S(1)}, u32[]{:S(2)}, u32[]{:S(2)}) collective-permute-start(bf16[256,512]{0,1:T(8,128)(2,1)S(1)} %collective-permute-done.6), channel_id=1, source_target_pairs={{0,1},{1,2},{2,3},{3,4},{4,5},{5,6},{6,7},{7,8},{8,9},{9,10},{10,1... | collective-permute-start | bytes 786440 | tf_op jit(solution)/shard_map/ppermute | solution.py:38
  184.7 5.6 %fusion.65 = (f32[2048]{0:T(1024)S(1)}, f32[2048,1280]{1,0:T(8,128)}) fusion(bf16[1280,4,128]{0,2,1:T(8,128)(2,1)S(1)} %bitcast.187, bf16[256,4,8,128]{3,2,1,0:T(8,128)(2,1)S(1)} %bitcast.177, pred[256,1280]{1,0:T(8,128)(4,1)S(1)} %compare_and_fusion), kind=kOutput, calls=%fused_computation.122 | convolution fusion | flops 678950912 | bytes 11673600 | tf_op jit(solution)/shard_map/dot_general | solution.py:56
  190.3 5.3 %fusion.66 = (f32[2048]{0:T(1024)S(1)}, f32[2048,1280]{1,0:T(8,128)}) fusion(bf16[1280,4,128]{0,2,1:T(8,128)(2,1)S(1)} %bitcast.188, bf16[256,4,8,128]{3,2,1,0:T(8,128)(2,1)S(1)} %bitcast.178, pred[256,1280]{1,0:T(8,128)(4,1)S(1)} %compare_and_fusion), kind=kOutput, calls=%fused_computation.123 | convolution fusion | flops 678950912 | bytes 11673600 | tf_op jit(solution)/shard_map/dot_general | solution.py:56
  195.6 5.1 %fusion.67 = (f32[2048]{0:T(1024)S(1)}, f32[2048,1280]{1,0:T(8,128)}) fusion(bf16[1280,4,128]{0,2,1:T(8,128)(2,1)S(1)} %bitcast.189, bf16[256,4,8,128]{3,2,1,0:T(8,128)(2,1)S(1)} %bitcast.179, pred[256,1280]{1,0:T(8,128)(4,1)S(1)} %compare_and_fusion), kind=kOutput, calls=%fused_computation.124 | convolution fusion | flops 678950912 | bytes 11673600 | tf_op jit(solution)/shard_map/dot_general | solution.py:56
  202.7 5.7 %fusion.4 = f32[2048]{0:T(1024)S(1)} fusion(f32[2048,1280]{1,0:T(8,128)} %get-tuple-element.126, f32[2048]{0:T(1024)S(1)} %get-tuple-element.125), kind=kLoop, calls=%fused_computation.25 | loop fusion | flops 5240832 | bytes 10502144 | tf_op jit(solution)/shard_map/reduce_sum | solution.py:63
  208.5 6.0 %fusion.58 = bf16[256,1,8,128]{3,2,0,1:T(8,128)(2,1)S(1)} fusion(f32[2048,1280]{1,0:T(8,128)} %copy-done.2, f32[2048]{0:T(1024)S(1)} %get-tuple-element.123, f32[256,8]{1,0:T(8,128)S(1)} %div.49, bf16[1280,4,128]{0,2,1:T(8,128)(2,1)S(1)} %bitcast.199), kind=kOutput, calls=%fused_computation.59 | convolution fusion | flops 676855808 | bytes 11476992 | tf_op jit(solution)/shard_map/dot_general | solution.py:65
  214.5 6.0 %fusion.49 = bf16[256,1,8,128]{3,2,0,1:T(8,128)(2,1)S(1)} fusion(f32[2048,1280]{1,0:T(8,128)} %get-tuple-element.126, f32[2048]{0:T(1024)S(1)} %get-tuple-element.125, f32[256,8]{1,0:T(8,128)S(1)} %div.46, bf16[1280,4,128]{0,2,1:T(8,128)(2,1)S(1)} %bitcast.200), kind=kOutput, calls=%fused_computation.56 | convolution fusion | flops 676855808 | bytes 11476992 | tf_op jit(solution)/shard_map/dot_general | solution.py:65
  222.4 5.8 %fusion.40 = bf16[256,1,8,128]{3,2,0,1:T(8,128)(2,1)S(1)} fusion(f32[2048,1280]{1,0:T(8,128)} %get-tuple-element.128, f32[2048]{0:T(1024)S(1)} %get-tuple-element.127, f32[256,8]{1,0:T(8,128)S(1)} %div.43, bf16[1280,4,128]{0,2,1:T(8,128)(2,1)S(1)} %bitcast.201), kind=kOutput, calls=%fused_computation.53 | convolution fusion | flops 676855808 | bytes 11476992 | tf_op jit(solution)/shard_map/dot_general | solution.py:65
  228.2 5.9 %fusion = f32[2048]{0:T(1024)S(1)} fusion(f32[2048,1280]{1,0:T(8,128)} %get-tuple-element.130, f32[2048]{0:T(1024)S(1)} %get-tuple-element.129), kind=kLoop, calls=%fused_computation.21 | loop fusion | flops 5240832 | bytes 10502144 | tf_op jit(solution)/shard_map/reduce_sum | solution.py:63
  234.2 5.8 %fusion.31 = bf16[256,1,8,128]{3,2,0,1:T(8,128)(2,1)S(1)} fusion(f32[2048,1280]{1,0:T(8,128)} %get-tuple-element.130, f32[2048]{0:T(1024)S(1)} %get-tuple-element.129, f32[256,8]{1,0:T(8,128)S(1)} %div.40, bf16[1280,4,128]{0,2,1:T(8,128)(2,1)S(1)} %bitcast.202), kind=kOutput, calls=%fused_computation.50 | convolution fusion | flops 676855808 | bytes 11476992 | tf_op jit(solution)/shard_map/dot_general | solution.py:65
  248.6 4.1 %collective-permute-start.15 = (f32[8]{0:T(128)S(1)}, f32[8]{0:T(128)S(1)}, u32[]{:S(2)}, u32[]{:S(2)}) collective-permute-start(f32[8]{0:T(128)S(1)} %select_reduce_fusion), channel_id=1, source_target_pairs={{0,1},{1,0},{2,3},{3,2},{4,5},{5,4},{6,7},{7,6},{8,9},{9,8},{10,11... | collective-permute-start | bytes 104 | tf_op jit(solution)/shard_map/ppermute | solution.py:18
  253.5 3.7 %collective-permute-start.16 = (f32[8]{0:T(128)S(1)}, f32[8]{0:T(128)S(1)}, u32[]{:S(2)}, u32[]{:S(2)}) collective-permute-start(f32[8]{0:T(128)S(1)} %add.147), channel_id=1, source_target_pairs={{0,2},{1,3},{2,0},{3,1},{4,6},{5,7},{6,4},{7,5},{8,10},{9,11},{10,... | collective-permute-start | bytes 104 | tf_op jit(solution)/shard_map/ppermute | solution.py:18
  258.7 23.3 %collective-permute-start.17 = (f32[8]{0:T(128)S(1)}, f32[8]{0:T(128)S(1)}, u32[]{:S(2)}, u32[]{:S(2)}) collective-permute-start(f32[8]{0:T(128)S(1)} %add.148), channel_id=1, source_target_pairs={{0,4},{1,5},{2,6},{3,7},{4,0},{5,1},{6,2},{7,3},{8,12},{9,13},{10,... | collective-permute-start | bytes 104 | tf_op jit(solution)/shard_map/ppermute | solution.py:18
  283.6 5.6 %collective-permute-start.18 = (f32[8]{0:T(128)S(1)}, f32[8]{0:T(128)S(1)}, u32[]{:S(2)}, u32[]{:S(2)}) collective-permute-start(f32[8]{0:T(128)S(1)} %add.149), channel_id=1, source_target_pairs={{0,8},{1,9},{2,10},{3,11},{4,12},{5,13},{6,14},{7,15},{8,0},{9,1},... | collective-permute-start | bytes 104 | tf_op jit(solution)/shard_map/ppermute | solution.py:18
  (135 shorter events, 70.2 us)
Async XLA Ops:
  0.6 26.5 %copy-start = (bf16[768,512]{1,0:T(8,128)(2,1)S(1)}, bf16[768,512]{1,0:T(8,128)(2,1)}, u32[]{:S(2)}) copy-start(bf16[768,512]{1,0:T(8,128)(2,1)} %param.14) | copy-start | bytes 2359300
  4.6 150.6 %collective-permute-start.14 = (s32[1]{0:T(128)}, s32[1]{0:T(128)}, u32[]{:S(2)}, u32[]{:S(2)}) collective-permute-start(s32[1]{0:T(128)} %add.146), channel_id=1, source_target_pairs={{1,0},{2,1},{3,2},{4,3},{5,4},{6,5},{7,6},{8,7},{9,8},{10,9},{11,1... | collective-permute-start | bytes 20 | tf_op jit(solution)/shard_map/ppermute | solution.py:38
  30.4 50.0 %collective-permute-start.2 = (bf16[256,512]{0,1:T(8,128)(2,1)}, bf16[256,512]{0,1:T(8,128)(2,1)}, u32[]{:S(2)}, u32[]{:S(2)}) collective-permute-start(bf16[256,512]{0,1:T(8,128)(2,1)} %copy.48), channel_id=1, source_target_pairs={{0,1},{1,2},{2,3},{3,4},{4,5},{5,6},{6,7},{7,8},{8,9},{9,10},{10,1... | collective-permute-start | bytes 786440 | tf_op jit(solution)/shard_map/ppermute | solution.py:38
  36.3 29.5 %collective-permute-start.8 = (bf16[256,512]{0,1:T(8,128)(2,1)S(1)}, bf16[256,512]{0,1:T(8,128)(2,1)}, u32[]{:S(2)}, u32[]{:S(2)}) collective-permute-start(bf16[256,512]{0,1:T(8,128)(2,1)S(1)} %copy.52), channel_id=1, source_target_pairs={{0,1},{1,2},{2,3},{3,4},{4,5},{5,6},{6,7},{7,8},{8,9},{9,10},{10,1... | collective-permute-start | bytes 786440 | tf_op jit(solution)/shard_map/ppermute | solution.py:38
  51.3 41.1 %collective-permute-start.3 = (bf16[256,512]{0,1:T(8,128)(2,1)}, bf16[256,512]{0,1:T(8,128)(2,1)}, u32[]{:S(2)}, u32[]{:S(2)}) collective-permute-start(bf16[256,512]{0,1:T(8,128)(2,1)} %copy.50), channel_id=1, source_target_pairs={{1,0},{2,1},{3,2},{4,3},{5,4},{6,5},{7,6},{8,7},{9,8},{10,9},{11,1... | collective-permute-start | bytes 786440 | tf_op jit(solution)/shard_map/ppermute | solution.py:38
  53.4 13.8 %collective-permute-start.9 = (bf16[256,512]{0,1:T(8,128)(2,1)}, bf16[256,512]{0,1:T(8,128)(2,1)}, u32[]{:S(2)}, u32[]{:S(2)}) collective-permute-start(bf16[256,512]{0,1:T(8,128)(2,1)} %copy.54), channel_id=1, source_target_pairs={{1,0},{2,1},{3,2},{4,3},{5,4},{6,5},{7,6},{8,7},{9,8},{10,9},{11,1... | collective-permute-start | bytes 786440 | tf_op jit(solution)/shard_map/ppermute | solution.py:38
  65.9 112.8 %collective-permute-start.1 = (bf16[256,4096]{1,0:T(8,128)(2,1)}, bf16[256,4096]{1,0:T(8,128)(2,1)}, u32[]{:S(2)}, u32[]{:S(2)}) collective-permute-start(bf16[256,4096]{1,0:T(8,128)(2,1)} %bitcast.184), channel_id=1, source_target_pairs={{1,0},{2,1},{3,2},{4,3},{5,4},{6,5},{7,6},{8,7},{9,8},{10,9},{11,1... | collective-permute-start | bytes 6291464 | tf_op jit(solution)/shard_map/ppermute | solution.py:38
  68.3 30.0 %collective-permute-start.10 = (bf16[256,512]{0,1:T(8,128)(2,1)S(1)}, bf16[256,512]{0,1:T(8,128)(2,1)S(1)}, u32[]{:S(2)}, u32[]{:S(2)}) collective-permute-start(bf16[256,512]{0,1:T(8,128)(2,1)S(1)} %add_add_fusion), channel_id=1, source_target_pairs={{0,1},{1,2},{2,3},{3,4},{4,5},{5,6},{6,7},{7,8},{8,9},{9,10},{10,1... | collective-permute-start | bytes 786440 | tf_op jit(solution)/shard_map/ppermute | solution.py:38
  80.4 98.3 %collective-permute-start = (bf16[256,4096]{1,0:T(8,128)(2,1)}, bf16[256,4096]{1,0:T(8,128)(2,1)}, u32[]{:S(2)}, u32[]{:S(2)}) collective-permute-start(bf16[256,4096]{1,0:T(8,128)(2,1)} %bitcast.185), channel_id=1, source_target_pairs={{0,1},{1,2},{2,3},{3,4},{4,5},{5,6},{6,7},{7,8},{8,9},{9,10},{10,1... | collective-permute-start | bytes 6291464 | tf_op jit(solution)/shard_map/ppermute | solution.py:38
  93.5 53.6 %copy-start.9 = (s32[256]{0:T(256)S(1)}, s32[256]{0:T(256)}, u32[]{:S(2)}) copy-start(s32[256]{0:T(256)} %param.16) | copy-start | bytes 3076
  93.5 17.2 %collective-permute-start.4 = (bf16[256,512]{0,1:T(8,128)(2,1)S(1)}, bf16[256,512]{0,1:T(8,128)(2,1)S(1)}, u32[]{:S(2)}, u32[]{:S(2)}) collective-permute-start(bf16[256,512]{0,1:T(8,128)(2,1)S(1)} %add_add_fusion.1), channel_id=1, source_target_pairs={{0,1},{1,2},{2,3},{3,4},{4,5},{5,6},{6,7},{7,8},{8,9},{9,10},{10,1... | collective-permute-start | bytes 786440 | tf_op jit(solution)/shard_map/ppermute | solution.py:38
  98.3 44.3 %collective-permute-start.11 = (bf16[256,512]{0,1:T(8,128)(2,1)S(1)}, bf16[256,512]{0,1:T(8,128)(2,1)S(1)}, u32[]{:S(2)}, u32[]{:S(2)}) collective-permute-start(bf16[256,512]{0,1:T(8,128)(2,1)S(1)} %collective-permute-done.10), channel_id=1, source_target_pairs={{0,1},{1,2},{2,3},{3,4},{4,5},{5,6},{6,7},{7,8},{8,9},{9,10},{10,1... | collective-permute-start | bytes 786440 | tf_op jit(solution)/shard_map/ppermute | solution.py:38
  110.6 39.7 %copy-start.4 = (bf16[256,512]{0,1:T(8,128)(2,1)}, bf16[256,512]{0,1:T(8,128)(2,1)S(1)}, u32[]{:S(2)}) copy-start(bf16[256,512]{0,1:T(8,128)(2,1)S(1)} %collective-permute-done.4) | copy-start | bytes 786436
  110.6 36.5 %collective-permute-start.5 = (bf16[256,512]{0,1:T(8,128)(2,1)S(1)}, bf16[256,512]{0,1:T(8,128)(2,1)S(1)}, u32[]{:S(2)}, u32[]{:S(2)}) collective-permute-start(bf16[256,512]{0,1:T(8,128)(2,1)S(1)} %collective-permute-done.4), channel_id=1, source_target_pairs={{0,1},{1,2},{2,3},{3,4},{4,5},{5,6},{6,7},{7,8},{8,9},{9,10},{10,1... | collective-permute-start | bytes 786440 | tf_op jit(solution)/shard_map/ppermute | solution.py:38
  142.7 7.7 %collective-permute-start.12 = (bf16[256,512]{0,1:T(8,128)(2,1)S(1)}, bf16[256,512]{0,1:T(8,128)(2,1)S(1)}, u32[]{:S(2)}, u32[]{:S(2)}) collective-permute-start(bf16[256,512]{0,1:T(8,128)(2,1)S(1)} %collective-permute-done.11), channel_id=1, source_target_pairs={{0,1},{1,2},{2,3},{3,4},{4,5},{5,6},{6,7},{7,8},{8,9},{9,10},{10,1... | collective-permute-start | bytes 786440 | tf_op jit(solution)/shard_map/ppermute | solution.py:38
  147.1 8.8 %collective-permute-start.6 = (bf16[256,512]{0,1:T(8,128)(2,1)S(1)}, bf16[256,512]{0,1:T(8,128)(2,1)S(1)}, u32[]{:S(2)}, u32[]{:S(2)}) collective-permute-start(bf16[256,512]{0,1:T(8,128)(2,1)S(1)} %collective-permute-done.5), channel_id=1, source_target_pairs={{0,1},{1,2},{2,3},{3,4},{4,5},{5,6},{6,7},{7,8},{8,9},{9,10},{10,1... | collective-permute-start | bytes 786440 | tf_op jit(solution)/shard_map/ppermute | solution.py:38
  150.4 26.9 %collective-permute-start.13 = (bf16[256,512]{0,1:T(8,128)(2,1)S(1)}, bf16[256,512]{0,1:T(8,128)(2,1)S(1)}, u32[]{:S(2)}, u32[]{:S(2)}) collective-permute-start(bf16[256,512]{0,1:T(8,128)(2,1)S(1)} %collective-permute-done.12), channel_id=1, source_target_pairs={{0,1},{1,2},{2,3},{3,4},{4,5},{5,6},{6,7},{7,8},{8,9},{9,10},{10,1... | collective-permute-start | bytes 786440 | tf_op jit(solution)/shard_map/ppermute | solution.py:38
  155.9 22.7 %collective-permute-start.7 = (bf16[256,512]{0,1:T(8,128)(2,1)S(1)}, bf16[256,512]{0,1:T(8,128)(2,1)S(1)}, u32[]{:S(2)}, u32[]{:S(2)}) collective-permute-start(bf16[256,512]{0,1:T(8,128)(2,1)S(1)} %collective-permute-done.6), channel_id=1, source_target_pairs={{0,1},{1,2},{2,3},{3,4},{4,5},{5,6},{6,7},{7,8},{8,9},{9,10},{10,1... | collective-permute-start | bytes 786440 | tf_op jit(solution)/shard_map/ppermute | solution.py:38
  178.6 35.9 %copy-start.7 = (bf16[1280,512]{0,1:T(8,128)(2,1)}, bf16[1280,512]{0,1:T(8,128)(2,1)S(1)}, u32[]{:S(2)}) copy-start(bf16[1280,512]{0,1:T(8,128)(2,1)S(1)} %constant_dynamic-update-slice_fusion.5) | copy-start | bytes 3932164
  244.6 46.6 %copy-start.1 = (bf16[768,512]{1,0:T(8,128)(2,1)S(1)}, bf16[768,512]{1,0:T(8,128)(2,1)}, u32[]{:S(2)}) copy-start(bf16[768,512]{1,0:T(8,128)(2,1)} %param.14) | copy-start | bytes 2359300
  248.6 4.9 %collective-permute-start.15 = (f32[8]{0:T(128)S(1)}, f32[8]{0:T(128)S(1)}, u32[]{:S(2)}, u32[]{:S(2)}) collective-permute-start(f32[8]{0:T(128)S(1)} %select_reduce_fusion), channel_id=1, source_target_pairs={{0,1},{1,0},{2,3},{3,2},{4,5},{5,4},{6,7},{7,6},{8,9},{9,8},{10,11... | collective-permute-start | bytes 104 | tf_op jit(solution)/shard_map/ppermute | solution.py:18
  253.5 5.2 %collective-permute-start.16 = (f32[8]{0:T(128)S(1)}, f32[8]{0:T(128)S(1)}, u32[]{:S(2)}, u32[]{:S(2)}) collective-permute-start(f32[8]{0:T(128)S(1)} %add.147), channel_id=1, source_target_pairs={{0,2},{1,3},{2,0},{3,1},{4,6},{5,7},{6,4},{7,5},{8,10},{9,11},{10,... | collective-permute-start | bytes 104 | tf_op jit(solution)/shard_map/ppermute | solution.py:18
  258.7 24.8 %collective-permute-start.17 = (f32[8]{0:T(128)S(1)}, f32[8]{0:T(128)S(1)}, u32[]{:S(2)}, u32[]{:S(2)}) collective-permute-start(f32[8]{0:T(128)S(1)} %add.148), channel_id=1, source_target_pairs={{0,4},{1,5},{2,6},{3,7},{4,0},{5,1},{6,2},{7,3},{8,12},{9,13},{10,... | collective-permute-start | bytes 104 | tf_op jit(solution)/shard_map/ppermute | solution.py:18
  283.6 7.2 %collective-permute-start.18 = (f32[8]{0:T(128)S(1)}, f32[8]{0:T(128)S(1)}, u32[]{:S(2)}, u32[]{:S(2)}) collective-permute-start(f32[8]{0:T(128)S(1)} %add.149), channel_id=1, source_target_pairs={{0,8},{1,9},{2,10},{3,11},{4,12},{5,13},{6,14},{7,15},{8,0},{9,1},... | collective-permute-start | bytes 104 | tf_op jit(solution)/shard_map/ppermute | solution.py:18
  (9 other events, 83.0 us)
